TPU v7x, 32 devices: a whole 2x2x4 slice. The times are simulated.
32 devices in a mesh: dp: 2 (over core), tvoc: 4 (over y, x), svoc: 4 (over z).
Axes of the slice: x: 2, y: 2, z: 4, core: 2. Of those that a mesh axis runs over, the one named last changes fastest.
Arguments:
- teacher_probs: bfloat16 [256, 20480], P('dp', 'tvoc'), may hold values from 0 to 1, as said below
- block_values: bfloat16 [4, 4, 24, 128, 128], P('tvoc', 'svoc'), may hold values from 0.0099487305 to 1
- block_index: int32 [4, 4, 24, 2], P('tvoc', 'svoc'), may hold values from 0 to 39, as said below
- block_count: int32 [4, 4], P('tvoc', 'svoc'), may hold values from 5 to 24, as said below
- hidden: bfloat16 [256, 3072], P('dp'), may hold values from -48 to 48
- student_weight: bfloat16 [3072, 8192], P(None, ('tvoc', 'svoc')), may hold values from -0.15 to 0.15
Outputs:
- divergence: float32 [256], P('dp')
- grad_weight: bfloat16 [3072, 8192], P('dp', ('tvoc', 'svoc'))
- grad_hidden: float32 [256, 3072], P('dp', ('tvoc', 'svoc'))
Inputs may be any that keep to these rules, and one draw needn't show every extreme that they name: `teacher_probs`: each row sums to one and every entry is positive. `block_index`: The live slots of one device name at most 2 distinct c with the same c // 4, and some value of c // 4 reaches 2 on every device. Several live slots may name the same c, with the same or another teacher block. `block_count`: the live slots are the first ones; some device has all 24 live.
All inputs are finite; a program needn't handle non-finite values.
Results may differ from a plain program's by a relative error of at most 0.013.
Values may be sent and summed in bfloat16 or wider, within the bound.
A program may use at most 64 MiB of HBM per device.

v0:
```python
import jax
import jax.numpy as jnp
from jax import lax
from jax.sharding import PartitionSpec as P

loss_scale = 128.0


def local(teacher_probs, block_values, block_index, block_count, hidden, student_weight):
    tokens = hidden.shape[0]
    block_size = block_values.shape[-1]
    slot_count = block_values.shape[2]
    owners = lax.axis_size("tvoc")
    shard_width = student_weight.shape[1]
    per_owner = shard_width // block_size
    teacher_rows = block_index[0, 0, :, 0]
    block_columns = block_index[0, 0, :, 1]
    occupied = jnp.arange(slot_count, dtype=jnp.int32) < block_count[0, 0]
    teacher_blocks = teacher_probs.reshape(tokens, -1, block_size)
    picked = jnp.take(teacher_blocks, teacher_rows, axis=1)
    mapped = jnp.einsum(
        "tsk,skc->stc", picked, block_values[0, 0], preferred_element_type=jnp.float32
    )
    select = (
        (block_columns[:, None] == jnp.arange(owners * per_owner, dtype=jnp.int32)[None, :])
        & occupied[:, None]
    ).astype(jnp.float32)
    partial_sum = jnp.einsum("sb,stc->tbc", select, mapped)
    partial_sum = partial_sum.reshape(tokens, owners, per_owner * block_size)
    rounded = lax.optimization_barrier(partial_sum.astype(jnp.bfloat16)).astype(jnp.float32)
    teacher_mass = (
        lax.psum_scatter(rounded.astype(jnp.bfloat16), "tvoc", scatter_dimension=1, tiled=True)
        .astype(jnp.float32)
        .reshape(tokens, shard_width)
    )
    logits = jnp.dot(hidden, student_weight, preferred_element_type=jnp.float32)
    positive = teacher_mass > 0
    entropy_local = jnp.sum(
        jnp.where(positive, teacher_mass * jnp.log(jnp.where(positive, teacher_mass, 1.0)), 0.0),
        axis=1,
    )
    cross_local = jnp.sum(teacher_mass * logits, axis=1)
    mass_local = jnp.sum(teacher_mass, axis=1)
    largest = lax.pmax(jnp.max(logits, axis=1), ("tvoc", "svoc"))
    shifted = jnp.exp(logits - largest[:, None])
    total, mass_sum, entropy_sum, cross_sum = lax.psum(
        (jnp.sum(shifted, axis=1), mass_local, entropy_local, cross_local), ("tvoc", "svoc")
    )
    divergence = (
        entropy_sum / mass_sum - jnp.log(mass_sum) - cross_sum / mass_sum + largest + jnp.log(total)
    )
    target = teacher_mass / mass_sum[:, None]
    logit_grad = (loss_scale * (shifted / total[:, None] - target)).astype(jnp.bfloat16)
    grad_weight = lax.psum_scatter(
        lax.dot_general(
            hidden, logit_grad, (((0,), (0,)), ((), ())), preferred_element_type=jnp.float32
        ).astype(jnp.bfloat16),
        "dp",
        scatter_dimension=0,
        tiled=True,
    )
    grad_hidden = lax.psum_scatter(
        lax.dot_general(
            student_weight, logit_grad, (((1,), (1,)), ((), ())), preferred_element_type=jnp.float32
        ),
        ("tvoc", "svoc"),
        scatter_dimension=0,
        tiled=True,
    ).T
    return (divergence, grad_weight, grad_hidden)


def solution(mesh):
    return jax.shard_map(
        local,
        mesh=mesh,
        in_specs=(
            P("dp", "tvoc"),
            P("tvoc", "svoc", None, None, None),
            P("tvoc", "svoc", None, None),
            P("tvoc", "svoc"),
            P("dp", None),
            P(None, ("tvoc", "svoc")),
        ),
        out_specs=(P("dp"), P("dp", ("tvoc", "svoc")), P("dp", ("tvoc", "svoc"))),
        check_vma=False,
    )
```

profile of v0, /device:TPU:0, one launch (start us, length us, event | category | flops | bytes accessed | tf_op | source)
XLA Modules:
  0.0 262.2 jit_solution(12176187835906200167)
XLA Ops:
  7.2 0.8 fusion.30
  8.1 0.8 slice_bitcast_fusion
  8.8 0.7 compare_and_fusion
  10.2 2.4 copy.21
  12.6 2.4 copy.22
  15.0 2.9 %gather_fusion = bf16[24,128,128]{2,1,0:T(8,128)(2,1)} fusion(bf16[128,40,128]{2,0,1:T(8,128)(2,1)} %copy.22, s32[1024]{0:T(1024)S(1)} %pad_clamp_fusion), kind=kCustom, calls=%fused_computation | custom fusion | bytes 1572960 | tf_op jit(solution)/shard_map/jit(_take)/gather | solution.py:20
  17.9 1.8 fusion.9
  19.7 1.3 fusion.6
  21.0 2.0 convert_element_type.26
  23.1 1.9 copy.24
  25.0 0.0 reduce-scatter.8.cloned.1.call-start
  25.1 1.8 fusion.34
  26.9 43.8 %pmax.7 = f32[128]{0:T(128)S(1)} all-reduce(f32[128]{0:T(128)S(1)} %get-tuple-element.22), channel_id=1, replica_groups=mesh['dp'=2,'tvoc'=4,'svoc'=4] {'tvoc','svoc'}, use_global_device_ids=true, to_apply=%region_8.9 | all-reduce | flops 128 | bytes 1024 | tf_op jit(solution)/shard_map/pmax | solution.py:44
  70.6 1.0 convert_reduce_fusion
  71.7 1.1 fusion.18
  72.8 37.2 %all-reduce.1 = (f32[128]{0:T(128)S(1)}, f32[128]{0:T(128)S(1)}, f32[128]{0:T(128)S(1)}, f32[128]{0:T(128)}) all-reduce(f32[128]{0:T(128)S(1)} %get-tuple-element.16, f32[128]{0:T(128)S(1)} %get-tuple-element.15, f32[128]{0:T(128)S(1)} %convert_reduce_fusion, ...), channel_id=1, replica_groups=mesh['dp'=2,'tvoc'=4,'svoc'=4] {'tvoc','svoc'}, use_global_device_ids=true, to_apply=%region_10.11 | all-reduce | flops 512 | bytes 4096 | tf_op jit(solution)/shard_map/psum | solution.py:46
  110.0 4.0 %fusion = bf16[3072,512]{0,1:T(8,128)(2,1)} fusion(bf16[128,3072]{1,0:T(8,128)(2,1)} %param.10, bf16[128,1,512]{2,0,1:T(8,128)(2,1)} %reduce-scatter.12.cloned.1.call-done, f32[128,512]{1,0:T(8,128)S(1)} %get-tuple-element.23, f32[128]{0:T(128)S(1)} %get-tuple-element.20, f32[128]{0:T(128)S(1)} %get-tuple-element.18, f32[128]{0:T(128)S(1)} %pmax.7), kind=kOutput, calls=%fused_computation.2 | convolution fusion | flops 404684800 | bytes 4326912 | tf_op jit(solution)/shard_map/dot_general | solution.py:55
  114.1 0.0 reduce-scatter.10.cloned.1.call-start
  114.1 2.3 convolution_bitcast_fusion
  116.4 3.1 %copy.27 = f32[3072,128]{1,0:T(8,128)} copy(f32[3072,128]{0,1:T(8,128)} %convolution_bitcast_fusion) | data formatting | bytes 3145728
  119.6 0.5 log_add_fusion
  120.1 2.9 %reduce-scatter.8.cloned.1.call-done = bf16[1536,512]{0,1:T(8,128)(2,1)} async-done(((bf16[3072,512]{0,1:T(8,128)(2,1)}), bf16[1536,512]{0,1:T(8,128)(2,1)}) %reduce-scatter.8.cloned.1.call-update) | async-done | bytes 1572880 | tf_op jit(solution)/shard_map/reduce_scatter | solution.py:54
  123.0 2.6 copy.25
  125.6 130.2 %reduce-scatter.10.cloned.1.call-done = f32[192,128]{1,0:T(8,128)} async-done(((f32[3072,128]{1,0:T(8,128)}), f32[192,128]{1,0:T(8,128)}) %reduce-scatter.10.cloned.1.call-update) | async-done | bytes 98320
  (13 shorter events, 0.1 us)
Async XLA Ops:
  7.2 17.9 %copy-start = (bf16[3072,512]{1,0:T(8,128)(2,1)S(1)}, bf16[3072,512]{1,0:T(8,128)(2,1)}, u32[]{:S(2)}) copy-start(bf16[3072,512]{1,0:T(8,128)(2,1)} %param.11) | copy-start | bytes 9437188
  7.2 63.5 %reduce-scatter.12.cloned.1.call-start = ((), (), s32[]{:S(2)}) async-start(), calls=%async_computation.5 | async-start | bytes 655360
  25.0 98.0 %reduce-scatter.8.cloned.1.call-start = ((), (), s32[]{:S(2)}) async-start(), calls=%async_computation.3 | async-start | bytes 4718592 | tf_op jit(solution)/shard_map/reduce_scatter | solution.py:54
  110.0 4.1 %copy-start.1 = (bf16[128,1,512]{2,0,1:T(8,128)(2,1)S(1)}, bf16[128,1,512]{2,0,1:T(8,128)(2,1)}, u32[]{:S(2)}) copy-start(bf16[128,1,512]{2,0,1:T(8,128)(2,1)} %reduce-scatter.12.cloned.1.call-done) | copy-start | bytes 393220
  114.1 141.6 %reduce-scatter.10.cloned.1.call-start = ((), (), s32[]{:S(2)}) async-start(), calls=%async_computation.4 | async-start | bytes 1671168
  116.4 3.1 %copy-start.2 = (f32[128]{0:T(128)S(1)}, f32[128]{0:T(128)}, u32[]{:S(2)}) copy-start(f32[128]{0:T(128)} %get-tuple-element.21) | copy-start | bytes 1540
Sparse Core Ops, SparseCore 0:
  25.1 27.8 reduce-scatter.11
  114.2 8.7 reduce-scatter.7
  128.3 127.3 reduce-scatter.9
where the time goes:
time: 263 us; the launch traced here: 262 us
  waiting for transfers between devices  133 us (51%)
  blocking collectives  81 us (31%)
  local copies, waits for them, and re-layouts  18.1 us (7%)
  between operations  14.5 us (6%)
  matrix products  11.2 us (4%)
  other arithmetic  4.18 us (2%)
    unnamed x5, waiting for transfers between devices  130 us
    pmax x1, blocking collectives, local(): largest = lax.pmax(jnp.max(logits, axis=1), ('tvoc', 'svoc'))  43.8 us
    psum x1, blocking collectives, local(): lax.psum((jnp.sum(shifted, axis=1), mass_local, entropy_local, cross_loca...  37.2 us
    unnamed x9, local copies, waits for them, and re-layouts  8.11 us
  transfers between devices with their start and end apart: 3, of which 2 were waited for; matrix products, arithmetic and copies ran while one was open for 4% of the time, Pallas kernels for 0%

commit v1 on v0

v1 whole, which is shorter than its diff:
```python
import functools

import jax
import jax.numpy as jnp
from jax import lax
from jax.experimental import pallas as pl
from jax.experimental.pallas import tpu as pltpu
from jax.sharding import PartitionSpec as P

loss_scale = 128.0
cap = 2
tag_rows = 16
MESH = pl.DeviceIdType.MESH
f32, bf16 = jnp.float32, jnp.bfloat16


def packer(
    n_t, per_owner, idx_s, cnt_s, idx_v, teacher_hbm, values_hbm,
    packed, teacher, values, mapped, targets, tags, load_sem,
):
    tokens = teacher.shape[0]
    slots, blk = values.shape[0], values.shape[1]
    loads = (
        pltpu.make_async_copy(teacher_hbm, teacher, load_sem.at[0]),
        pltpu.make_async_copy(values_hbm.at[0, 0], values, load_sem.at[1]),
    )
    for load in loads:
        load.start()

    lanes = targets.shape[1]
    lane = lax.broadcasted_iota(jnp.int32, (slots, lanes), 1)
    slot = lax.broadcasted_iota(jnp.int32, (slots, lanes), 0)
    hot = (idx_v[0, 0][:, 1:2] == lane) & (slot < cnt_s[0, 0])
    present = jnp.max(jnp.where(hot, 1.0, 0.0), axis=0, keepdims=True)
    r_iota = lax.broadcasted_iota(jnp.int32, (lanes, lanes), 0).astype(f32)
    c_iota = lax.broadcasted_iota(jnp.int32, (lanes, lanes), 1).astype(f32)
    r_own = jnp.floor((r_iota + 0.5) / per_owner)
    c_own = jnp.floor((c_iota + 0.5) / per_owner)
    below = jnp.where((r_own == c_own) & (r_iota < c_iota), 1.0, 0.0)
    rank = jnp.dot(jnp.broadcast_to(present, (8, lanes)), below, preferred_element_type=f32)[0:1]
    place = cap * c_own[0:1] + rank
    goal = jnp.sum(jnp.where(hot, place + 1.0, 0.0), axis=1, keepdims=True) - 1.0
    targets[...] = jnp.broadcast_to(goal, (slots, lanes))
    n_tags = tags.shape[0]
    t_iota = lax.broadcasted_iota(jnp.int32, (n_tags, lanes), 0).astype(f32)
    within = c_iota[0:1] - per_owner * c_own[0:1]
    tag = jnp.sum(jnp.where((present > 0.0) & (place == t_iota), within + 1.0, 0.0), axis=1, keepdims=True) - 1.0
    tags[...] = jnp.broadcast_to(tag, (n_tags, lanes))

    for load in loads:
        load.wait()
    for s in range(slots):
        row = idx_s[0, 0, s, 0]
        picked = teacher[:, pl.ds(pl.multiple_of(row * blk, blk), blk)]
        mapped[s] = jnp.dot(picked, values[s], preferred_element_type=f32)

    def pack(o):
        for k in range(cap):
            t = (o * cap + k).astype(f32)
            acc = jnp.zeros((tokens, blk), f32)
            for s in range(slots):
                acc = acc + jnp.where(targets[s:s + 1, 0:blk] == t, mapped[s], 0.0)
            packed[o, 0:tokens, k * blk:(k + 1) * blk] = acc.astype(bf16)
            packed[o, tokens:tokens + tag_rows, k * blk:(k + 1) * blk] = jnp.broadcast_to(
                tags[pl.ds(o * cap + k, 1), 0:blk], (tag_rows, blk)).astype(bf16)

    def step(o, carry):
        pack(o)
        return carry

    lax.fori_loop(0, n_t, step, 0)


def kernel(
    n_t, n_s, blk,
    packed, hidden_hbm, weight_hbm,
    div_ref, gw_ref, gh_ref,
    hidden, weight, peer_hidden, hid_t, landed, mass, logits, stats, grads, grad_t, gh_t, out1, in1, out2, in2,
    load_sem, ph_sem, pk_send, pk_recv, st_send, st_recv, lg_sem, s1, r1, s2, r2,
):
    d, i, j = lax.axis_index("dp"), lax.axis_index("tvoc"), lax.axis_index("svoc")
    n_d = 2
    n = n_t * n_s
    me = i * n_s + j
    other = n_d - 1 - d
    tokens, width = hidden.shape
    shard = weight.shape[1]
    per_owner = shard // blk
    half = width // n_d
    rows = width // n

    loads = [
        pltpu.make_async_copy(src, dst, load_sem.at[k])
        for k, (src, dst) in enumerate(
            ((hidden_hbm, hidden), (weight_hbm, weight))
        )
    ]
    for load in loads:
        load.start()

    def peer(q):
        r = lax.rem(me + q, n)
        return r, {"tvoc": r // n_s, "svoc": lax.rem(r, n_s)}

    barrier = pltpu.get_barrier_semaphore()

    def greet(q, carry):
        pl.semaphore_signal(barrier, inc=1, device_id=peer(q)[1], device_id_type=MESH)
        return carry

    lax.fori_loop(1, n, greet, 0)
    pl.semaphore_signal(barrier, inc=1, device_id={"dp": other}, device_id_type=MESH)

    for load in loads:
        load.wait()
    depth = 4 * blk
    logits[...] = jnp.zeros_like(logits)

    def logit_step(k, carry):
        at = pl.multiple_of(k * depth, depth)
        logits[...] += jnp.dot(hidden[:, pl.ds(at, depth)], weight[pl.ds(at, depth), :], preferred_element_type=f32)
        return carry

    lax.fori_loop(0, width // depth, logit_step, 0)

    pl.semaphore_wait(barrier, n)

    def hidden_copy():
        start = pl.multiple_of(other * half, blk)
        return pltpu.make_async_remote_copy(
            src_ref=hidden.at[:, pl.ds(start, half)], dst_ref=peer_hidden,
            send_sem=ph_sem.at[0], recv_sem=ph_sem.at[1],
            device_id={"dp": other}, device_id_type=MESH)

    def packed_copy(o, src):
        return pltpu.make_async_remote_copy(
            src_ref=packed.at[o], dst_ref=landed.at[src],
            send_sem=pk_send.at[o], recv_sem=pk_recv.at[src],
            device_id={"tvoc": o}, device_id_type=MESH)

    def pack_send(q, carry):
        o = lax.rem(i + q, n_t)
        packed_copy(o, i).start()
        return carry

    lax.fori_loop(1, n_t, pack_send, 0)
    hidden_copy().start()

    own_at = d * half

    def turn_own(k, carry):
        at = pl.multiple_of(k * blk, blk)
        tile = hidden[:, pl.ds(pl.multiple_of(own_at + at, blk), blk)].astype(f32)
        hid_t[pl.ds(at, blk), 0:tokens] = tile.T.astype(bf16)
        return carry

    lax.fori_loop(0, half // blk, turn_own, 0)

    def add_mass(ref, o, first):
        for b in range(per_owner):
            acc = jnp.zeros((tokens, blk), f32) if first else mass[:, b * blk:(b + 1) * blk]
            for k in range(cap):
                which = ref[o, tokens:tokens + 1, k * blk:(k + 1) * blk].astype(f32)
                part = ref[o, 0:tokens, k * blk:(k + 1) * blk].astype(f32)
                acc = acc + jnp.where(which == float(b), part, 0.0)
            mass[:, b * blk:(b + 1) * blk] = acc

    add_mass(packed, i, True)

    def take_mass(q, carry):
        o = lax.rem(i + q, n_t)
        packed_copy(o, o).wait_recv()
        add_mass(landed, o, False)
        return carry

    lax.fori_loop(1, n_t, take_mass, 0)

    lg = logits[...]
    tm = mass[...]
    top = jnp.max(lg, axis=1, keepdims=True)
    e = jnp.exp(lg - top)
    positive = tm > 0
    parts = (
        top,
        jnp.sum(e, axis=1, keepdims=True),
        jnp.sum(tm, axis=1, keepdims=True),
        jnp.sum(jnp.where(positive, tm * jnp.log(jnp.where(positive, tm, 1.0)), 0.0), axis=1, keepdims=True),
        jnp.sum(tm * lg, axis=1, keepdims=True),
    )
    spot = lax.broadcasted_iota(jnp.int32, (tokens, 128), 1)
    wide = jnp.zeros((tokens, 128), f32)
    for k, part in enumerate(parts):
        wide = jnp.where(spot == k, part, wide)
    stats[me] = wide.T[0:8]
    logits[...] = e

    def stat_copy(q, src):
        r, where = peer(q)
        return pltpu.make_async_remote_copy(
            src_ref=stats.at[me], dst_ref=stats.at[src],
            send_sem=st_send.at[q], recv_sem=st_recv.at[src],
            device_id=where, device_id_type=MESH)

    def stat_send(q, carry):
        stat_copy(q, me).start()
        return carry

    lax.fori_loop(1, n, stat_send, 0)

    hidden_copy().wait_recv()

    def turn_peer(k, carry):
        at = pl.multiple_of(k * blk, blk)
        hid_t[pl.ds(at, blk), tokens:2 * tokens] = peer_hidden[:, pl.ds(at, blk)].astype(f32).T.astype(bf16)
        return carry

    lax.fori_loop(0, half // blk, turn_peer, 0)

    def stat_wait(q, carry):
        stat_copy(q, peer(q)[0]).wait_recv()
        return carry

    lax.fori_loop(1, n, stat_wait, 0)
    st = stats[...]
    largest = jnp.max(st, axis=0)[0:1]
    scale = jnp.exp(st[:, 0:1, :] - largest[None])
    line = lax.broadcasted_iota(jnp.int32, st.shape, 1)
    sums = jnp.sum(jnp.where(line == 1, st * scale, st), axis=0)
    total, mass_sum, entropy, cross = sums[1:2], sums[2:3], sums[3:4], sums[4:5]
    div_ref[...] = entropy / mass_sum - jnp.log(mass_sum) - cross / mass_sum + largest + jnp.log(total)
    rows8 = lax.broadcasted_iota(jnp.int32, (128, tokens), 0)
    back = jnp.where(rows8 == 0, largest, jnp.where(rows8 == 1, loss_scale / total, loss_scale / mass_sum)).T
    factor = jnp.exp(top - back[:, 0:1]) * back[:, 1:2]
    g = logits[...] * factor - mass[...] * back[:, 2:3]
    grads[0:tokens, :] = g.astype(bf16)
    lg_copy = pltpu.make_async_remote_copy(
        src_ref=grads.at[pl.ds(0, tokens)], dst_ref=grads.at[pl.ds(tokens, tokens)],
        send_sem=lg_sem.at[0], recv_sem=lg_sem.at[1],
        device_id={"dp": other}, device_id_type=MESH)
    lg_copy.start()
    grad_t[...] = g.T.astype(bf16)

    tile = 2 * blk

    def gh_step(k, carry):
        at = pl.multiple_of(k * tile, tile)
        gh_t[pl.ds(at, tile), :] = jnp.dot(weight[pl.ds(at, tile), :], grad_t[...], preferred_element_type=f32)
        return carry

    lax.fori_loop(0, width // tile, gh_step, 0)

    def chunk(ii, jj):
        return gh_t[pl.ds(pl.multiple_of((ii * n_s + jj) * rows, 8), rows), :]

    def copy1(ii, jj, src):
        return pltpu.make_async_remote_copy(
            src_ref=out1.at[ii, jj], dst_ref=in1.at[src, jj],
            send_sem=s1.at[ii, jj], recv_sem=r1.at[src, jj],
            device_id={"tvoc": ii}, device_id_type=MESH)

    def copy2(jj, src):
        return pltpu.make_async_remote_copy(
            src_ref=out2.at[jj], dst_ref=in2.at[src],
            send_sem=s2.at[jj], recv_sem=r2.at[src],
            device_id={"svoc": jj}, device_id_type=MESH)

    def send1(p, carry):
        jj = lax.rem(j + p, n_s)

        def inner(q, c):
            ii = lax.rem(i + q, n_t)
            out1[ii, jj] = chunk(ii, jj).astype(bf16)
            copy1(ii, jj, i).start()
            return c

        return lax.fori_loop(1, n_t, inner, carry)

    lax.fori_loop(1, n_s + 1, send1, 0)

    lg_copy.wait_recv()

    def gw_step(k, carry):
        at = pl.multiple_of(k * blk, blk)
        gw_ref[pl.ds(at, blk), :] = jnp.dot(
            hid_t[pl.ds(at, blk), :], grads[...], preferred_element_type=f32).astype(bf16)
        return carry

    lax.fori_loop(0, half // blk, gw_step, 0)

    def gather1(jj):
        acc = chunk(i, jj)
        for q in range(1, n_t):
            ii = lax.rem(i + q, n_t)
            copy1(ii, jj, ii).wait_recv()
            acc = acc + in1[ii, jj].astype(f32)
        return acc

    def send2(p, carry):
        jj = lax.rem(j + p, n_s)
        out2[jj] = gather1(jj).astype(bf16)
        copy2(jj, j).start()
        return carry

    lax.fori_loop(1, n_s, send2, 0)
    acc = gather1(j)
    for p in range(1, n_s):
        jj = lax.rem(j + p, n_s)
        copy2(jj, jj).wait_recv()
        acc = acc + in2[jj].astype(f32)
    gh_ref[...] = acc

    hidden_copy().wait_send()
    lg_copy.wait_send()

    def drain_packed(q, carry):
        o = lax.rem(i + q, n_t)
        packed_copy(o, i).wait_send()
        return carry

    lax.fori_loop(1, n_t, drain_packed, 0)

    def drain_stats(q, carry):
        stat_copy(q, me).wait_send()
        return carry

    lax.fori_loop(1, n, drain_stats, 0)

    def drain1(p, carry):
        jj = lax.rem(j + p, n_s)

        def inner(q, c):
            copy1(lax.rem(i + q, n_t), jj, i).wait_send()
            return c

        return lax.fori_loop(1, n_t, inner, carry)

    lax.fori_loop(1, n_s + 1, drain1, 0)

    def drain2(p, carry):
        copy2(lax.rem(j + p, n_s), j).wait_send()
        return carry

    lax.fori_loop(1, n_s, drain2, 0)


def local(n_t, n_s, teacher_probs, block_values, block_index, block_count, hidden, student_weight):
    tokens, width = hidden.shape
    slots, blk = block_values.shape[2], block_values.shape[3]
    shard = student_weight.shape[1]
    half, rows, n = width // 2, width // (n_t * n_s), n_t * n_s
    lanes = -(-(n_t * (shard // blk)) // 128) * 128
    vmem, smem = pl.BlockSpec(memory_space=pltpu.VMEM), pl.BlockSpec(memory_space=pltpu.SMEM)
    hbm = pl.BlockSpec(memory_space=pltpu.HBM)
    DMA = pltpu.SemaphoreType.DMA
    parcel = (n_t, tokens + tag_rows, cap * blk)
    packed = pl.pallas_call(
        functools.partial(packer, n_t, shard // blk),
        out_shape=jax.ShapeDtypeStruct(parcel, bf16),
        in_specs=[smem, smem, vmem, hbm, hbm],
        out_specs=vmem,
        scratch_shapes=[
            pltpu.VMEM(teacher_probs.shape, bf16),
            pltpu.VMEM(block_values.shape[2:], bf16),
            pltpu.VMEM((slots, tokens, blk), f32),
            pltpu.VMEM((slots, lanes), f32),
            pltpu.VMEM((n_t * cap, lanes), f32),
            DMA((2,)),
        ],
        compiler_params=pltpu.CompilerParams(vmem_limit_bytes=32 * 1024 * 1024),
    )(block_index, block_count, block_index, teacher_probs, block_values)
    div, gw, gh = pl.pallas_call(
        functools.partial(kernel, n_t, n_s, blk),
        out_shape=(
            jax.ShapeDtypeStruct((1, tokens), f32),
            jax.ShapeDtypeStruct((half, shard), bf16),
            jax.ShapeDtypeStruct((rows, tokens), f32),
        ),
        in_specs=[vmem, hbm, hbm],
        out_specs=(vmem, vmem, vmem),
        scratch_shapes=[
            pltpu.VMEM(hidden.shape, bf16),
            pltpu.VMEM(student_weight.shape, bf16),
            pltpu.VMEM((tokens, half), bf16),
            pltpu.VMEM((half, 2 * tokens), bf16),
            pltpu.VMEM(parcel, bf16),
            pltpu.VMEM((tokens, shard), f32),
            pltpu.VMEM((tokens, shard), f32),
            pltpu.VMEM((n, 8, tokens), f32),
            pltpu.VMEM((2 * tokens, shard), bf16),
            pltpu.VMEM((shard, tokens), bf16),
            pltpu.VMEM((width, tokens), f32),
            pltpu.VMEM((n_t, n_s, rows, tokens), bf16),
            pltpu.VMEM((n_t, n_s, rows, tokens), bf16),
            pltpu.VMEM((n_s, rows, tokens), bf16),
            pltpu.VMEM((n_s, rows, tokens), bf16),
            DMA((2,)), DMA((2,)), DMA((n_t,)), DMA((n_t,)), DMA((n,)), DMA((n,)), DMA((2,)),
            DMA((n_t, n_s)), DMA((n_t, n_s)), DMA((n_s,)), DMA((n_s,)),
        ],
        compiler_params=pltpu.CompilerParams(
            collective_id=0, has_side_effects=True, vmem_limit_bytes=32 * 1024 * 1024),
    )(packed, hidden, student_weight)
    return div.reshape(tokens), gw, gh.T


def solution(mesh):
    return jax.shard_map(
        functools.partial(local, mesh.shape["tvoc"], mesh.shape["svoc"]),
        mesh=mesh,
        in_specs=(
            P("dp", "tvoc"),
            P("tvoc", "svoc", None, None, None),
            P("tvoc", "svoc", None, None),
            P("tvoc", "svoc"),
            P("dp", None),
            P(None, ("tvoc", "svoc")),
        ),
        out_specs=(P("dp"), P("dp", ("tvoc", "svoc")), P("dp", ("tvoc", "svoc"))),
        check_vma=False,
    )
```

time: 263 us -> 43.3 us (0.16)
  waiting for transfers between devices: 133 us -> 0 us
  blocking collectives: 81 us -> 0 us
  Pallas kernels: 0 us -> 34.4 us
  between operations: 14.5 us -> 1.31 us
  matrix products: 11.2 us -> 0 us
  local copies, waits for them, and re-layouts: 18.1 us -> 7.39 us
  other arithmetic: 4.18 us -> 0 us
    unnamed x5 -> x0, waiting for transfers between devices: 130 us -> none
    pmax x1 -> x0, blocking collectives: 43.8 us -> none  [local(): largest = lax.pmax(jnp.max(logits, axis=1), ('tvoc', 'svoc'))]
    psum x1 -> x0, blocking collectives: 37.2 us -> none  [local(): lax.psum((jnp.sum(shifted, axis=1), mass_local, entropy_local, cross_loca...]
    pallas_call x0 -> x2, Pallas kernels: none -> 34.4 us  [the longest x1 31.6 us: local(): pl.pallas_call(functools.partial(kernel, n_t, n_s, blk), out_shape=(jax.S...]
    dot_general x5 -> x0, matrix products: 11.2 us -> none  [the longest x1 4.02 us: local(): lax.dot_general(hidden, logit_grad, (((0,), (0,)), ((), ())), preferred_e...]
    reduce_scatter x1 -> x0, waiting for transfers between devices: 2.88 us -> none  [local(): lax.psum_scatter(lax.dot_general(hidden, logit_grad, (((0,), (0,)), ((),...]
    gather x1 -> x0, local copies, waits for them, and re-layouts: 2.87 us -> none  [local(): picked = jnp.take(teacher_blocks, teacher_rows, axis=1)]
    unnamed x9 -> x12, local copies, waits for them, and re-layouts: 8.11 us -> 7.39 us
  transfers between devices with their start and end apart: 3 -> 0, of which waited for: 2 -> 0; matrix products, arithmetic and copies ran while one was open for 4% -> 0% of each run, Pallas kernels for 0% -> 0%
where the time goes in v1:
time: 43.3 us; the launch traced here: 43.1 us
  Pallas kernels  34.4 us (79%)
  local copies, waits for them, and re-layouts  7.39 us (17%)
  between operations  1.31 us (3%)
    pallas_call x1, Pallas kernels, local(): pl.pallas_call(functools.partial(kernel, n_t, n_s, blk), out_shape=(jax.S...  31.6 us
    unnamed x12, local copies, waits for them, and re-layouts  7.39 us
    pallas_call x1, Pallas kernels, local(): pl.pallas_call(functools.partial(packer, n_t, shard // blk), out_shape=ja...  2.78 us

profile of v1, /device:TPU:0, one launch (start us, length us, event | category | flops | bytes accessed | tf_op | source)
XLA Modules:
  0.0 43.1 jit_solution(3664097100102155227)
XLA Ops:
  1.3 0.8 %copy.9.idx_s.idx_v = s32[1,1,24,2]{3,2,1,0:T(8,128)S(1)} copy(s32[1,1,24,2]{2,3,1,0:T(2,128)} %param.8) | data formatting | bytes 384 | tf_op args[2]
  2.0 0.0 copy-start.1
  2.0 1.3 %copy-done.1 = bf16[128,5120]{1,0:T(8,128)(2,1)S(1)} copy-done((bf16[128,5120]{1,0:T(8,128)(2,1)S(1)}, bf16[128,5120]{1,0:T(8,128)(2,1)}, u32[]{:S(2)}) %copy-start.1) | copy-done | bytes 1310744
  3.4 0.0 copy-start.3
  3.4 1.1 %copy-done.3 = bf16[1,1,24,128,128]{4,3,2,1,0:T(8,128)(2,1)S(1)} copy-done((bf16[1,1,24,128,128]{4,3,2,1,0:T(8,128)(2,1)S(1)}, bf16[1,1,24,128,128]{4,3,2,1,0:T(8,128)(2,1)}, u32[]{:S(2)}) %copy-start.3) | copy-done | bytes 786456
  4.5 0.0 copy-start.2
  4.5 2.8 %shard_map.85.packed = bf16[4,144,256]{2,1,0:T(8,128)(2,1)S(1)} custom-call(s32[1,1,24,2]{3,2,1,0:T(8,128)S(1)} %copy.9.idx_s.idx_v, s32[1,1]{1,0:T(1,128)S(6)} %copy.14.cnt_s, s32[1,1,24,2]{3,2,1,0:T(8,128)S(1)} %copy.9.idx_s.idx_v, bf16[128,5120]{1,0:T(8,128)(2,1)S(1)} %copy-done.1, bf16[1,1,24,128,128]{4,3,2,1,0:T(8,128)(2,1)S(1)} %copy-done.3), custom_call_target="tpu_custom_call" | custom-call | tf_op jit(solution)/shard_map/pallas_call | solution.py:356
  7.3 0.0 copy-done.2
  7.3 0.0 copy-start
  7.3 1.9 %copy-done = bf16[3072,512]{1,0:T(8,128)(2,1)S(1)} copy-done((bf16[3072,512]{1,0:T(8,128)(2,1)S(1)}, bf16[3072,512]{1,0:T(8,128)(2,1)}, u32[]{:S(2)}) %copy-start) | copy-done | bytes 3145752
  9.2 31.6 %shard_map.86 = (f32[1,128]{1,0:T(1,128)S(1)}, bf16[1536,512]{1,0:T(8,128)(2,1)S(1)}, f32[192,128]{1,0:T(8,128)S(1)}) custom-call(bf16[4,144,256]{2,1,0:T(8,128)(2,1)S(1)} %shard_map.85.packed, bf16[128,3072]{1,0:T(8,128)(2,1)S(1)} %copy-done.2, bf16[3072,512]{1,0:T(8,128)(2,1)S(1)} %copy-done), custom_call_target="tpu_custom_call" | custom-call | tf_op jit(solution)/shard_map/pallas_call | solution.py:371
  40.8 0.5 %copy.15 = f32[128]{0:T(128)} copy(f32[128]{0:T(128)S(1)} %bitcast.3) | data formatting | bytes 1024
  41.3 1.1 %copy.16 = bf16[1536,512]{1,0:T(8,128)(2,1)} copy(bf16[1536,512]{1,0:T(8,128)(2,1)S(1)} %get-tuple-element.13) | data formatting | bytes 3145728
  42.4 0.6 %copy.17 = f32[128,192]{0,1:T(8,128)} copy(f32[128,192]{0,1:T(8,128)S(1)} %bitcast.2) | data formatting | bytes 196608
Async XLA Ops:
  2.0 1.3 %copy-start.1 = (bf16[128,5120]{1,0:T(8,128)(2,1)S(1)}, bf16[128,5120]{1,0:T(8,128)(2,1)}, u32[]{:S(2)}) copy-start(bf16[128,5120]{1,0:T(8,128)(2,1)} %teacher_hbm.1) | copy-start | bytes 3932164
  3.4 1.1 %copy-start.3 = (bf16[1,1,24,128,128]{4,3,2,1,0:T(8,128)(2,1)S(1)}, bf16[1,1,24,128,128]{4,3,2,1,0:T(8,128)(2,1)}, u32[]{:S(2)}) copy-start(bf16[1,1,24,128,128]{4,3,2,1,0:T(8,128)(2,1)} %values_hbm.1) | copy-start | bytes 2359300
  4.5 2.8 %copy-start.2 = (bf16[128,3072]{1,0:T(8,128)(2,1)S(1)}, bf16[128,3072]{1,0:T(8,128)(2,1)}, u32[]{:S(2)}) copy-start(bf16[128,3072]{1,0:T(8,128)(2,1)} %hidden_hbm.1) | copy-start | bytes 2359300
  7.3 1.9 %copy-start = (bf16[3072,512]{1,0:T(8,128)(2,1)S(1)}, bf16[3072,512]{1,0:T(8,128)(2,1)}, u32[]{:S(2)}) copy-start(bf16[3072,512]{1,0:T(8,128)(2,1)} %weight_hbm.1) | copy-start | bytes 9437188

commit v2 on v1

--- a/solution.py
+++ b/solution.py
@@ -14,23 +14,64 @@
 f32, bf16 = jnp.float32, jnp.bfloat16
 
 
-def packer(
-    n_t, per_owner, idx_s, cnt_s, idx_v, teacher_hbm, values_hbm,
-    packed, teacher, values, mapped, targets, tags, load_sem,
+def kernel(
+    n_t, n_s, blk,
+    idx_s, cnt_s, teacher_hbm, values_hbm, hidden_hbm, weight_hbm,
+    div_ref, gw_ref, gh_ref,
+    teacher, values, hidden, weight, peer_hidden, hid_t, mapped, targets, tags,
+    packed, landed, mass, logits, shifted, stats, grads, grad_t, gh_t, own_t, out1, in1, out2, in2,
+    block_sem, load_sem, ph_sem, pk_send, pk_recv, st_send, st_recv, lg_sem, s1, r1, s2, r2,
 ):
-    tokens = teacher.shape[0]
-    slots, blk = values.shape[0], values.shape[1]
-    loads = (
-        pltpu.make_async_copy(teacher_hbm, teacher, load_sem.at[0]),
-        pltpu.make_async_copy(values_hbm.at[0, 0], values, load_sem.at[1]),
-    )
-    for load in loads:
-        load.start()
+    d, i, j = lax.axis_index("dp"), lax.axis_index("tvoc"), lax.axis_index("svoc")
+    n_d = 2
+    n = n_t * n_s
+    me = i * n_s + j
+    other = n_d - 1 - d
+    tokens, width = hidden.shape
+    shard = weight.shape[1]
+    per_owner = shard // blk
+    half = width // n_d
+    rows = width // n
+
+    slots, blocks = values.shape[0], teacher.shape[0]
+    loads = [
+        pltpu.make_async_copy(src, dst, load_sem.at[k])
+        for k, (src, dst) in enumerate(((values_hbm.at[0, 0], values), (hidden_hbm, hidden), (weight_hbm, weight)))
+    ]
+    loads[0].start()
+
+    def block_load(b):
+        return pltpu.make_async_copy(
+            teacher_hbm.at[:, pl.ds(pl.multiple_of(b * blk, blk), blk)], teacher.at[b], block_sem.at[b])
+
+    def block_start(b, carry):
+        block_load(b).start()
+        return carry
+
+    lax.fori_loop(0, blocks, block_start, 0)
+    loads[1].start()
+    loads[2].start()
+
+    def peer(q):
+        r = lax.rem(me + q, n)
+        return r, {"tvoc": r // n_s, "svoc": lax.rem(r, n_s)}
+
+    barrier = pltpu.get_barrier_semaphore()
+
+    def greet(q, carry):
+        pl.semaphore_signal(barrier, inc=1, device_id=peer(q)[1], device_id_type=MESH)
+        return carry
+
+    lax.fori_loop(1, n, greet, 0)
+    pl.semaphore_signal(barrier, inc=1, device_id={"dp": other}, device_id_type=MESH)
 
     lanes = targets.shape[1]
     lane = lax.broadcasted_iota(jnp.int32, (slots, lanes), 1)
     slot = lax.broadcasted_iota(jnp.int32, (slots, lanes), 0)
-    hot = (idx_v[0, 0][:, 1:2] == lane) & (slot < cnt_s[0, 0])
+    column = jnp.zeros((slots, lanes), jnp.int32)
+    for s in range(slots):
+        column = jnp.where(slot == s, idx_s[0, 0, 1, s], column)
+    hot = (column == lane) & (slot < cnt_s[0, 0])
     present = jnp.max(jnp.where(hot, 1.0, 0.0), axis=0, keepdims=True)
     r_iota = lax.broadcasted_iota(jnp.int32, (lanes, lanes), 0).astype(f32)
     c_iota = lax.broadcasted_iota(jnp.int32, (lanes, lanes), 1).astype(f32)
@@ -47,14 +88,17 @@
     tag = jnp.sum(jnp.where((present > 0.0) & (place == t_iota), within + 1.0, 0.0), axis=1, keepdims=True) - 1.0
     tags[...] = jnp.broadcast_to(tag, (n_tags, lanes))
 
-    for load in loads:
-        load.wait()
+    def block_wait(b, carry):
+        block_load(b).wait()
+        return carry
+
+    loads[0].wait()
+    lax.fori_loop(0, blocks, block_wait, 0)
     for s in range(slots):
-        row = idx_s[0, 0, s, 0]
-        picked = teacher[:, pl.ds(pl.multiple_of(row * blk, blk), blk)]
-        mapped[s] = jnp.dot(picked, values[s], preferred_element_type=f32)
-
-    def pack(o):
+        mapped[s] = jnp.dot(teacher[idx_s[0, 0, 0, s]], values[s], preferred_element_type=f32)
+
+    def pack(q, carry):
+        o = lax.rem(i + q, n_t)
         for k in range(cap):
             t = (o * cap + k).astype(f32)
             acc = jnp.zeros((tokens, blk), f32)
@@ -63,65 +107,9 @@
             packed[o, 0:tokens, k * blk:(k + 1) * blk] = acc.astype(bf16)
             packed[o, tokens:tokens + tag_rows, k * blk:(k + 1) * blk] = jnp.broadcast_to(
                 tags[pl.ds(o * cap + k, 1), 0:blk], (tag_rows, blk)).astype(bf16)
-
-    def step(o, carry):
-        pack(o)
-        return carry
-
-    lax.fori_loop(0, n_t, step, 0)
-
-
-def kernel(
-    n_t, n_s, blk,
-    packed, hidden_hbm, weight_hbm,
-    div_ref, gw_ref, gh_ref,
-    hidden, weight, peer_hidden, hid_t, landed, mass, logits, stats, grads, grad_t, gh_t, out1, in1, out2, in2,
-    load_sem, ph_sem, pk_send, pk_recv, st_send, st_recv, lg_sem, s1, r1, s2, r2,
-):
-    d, i, j = lax.axis_index("dp"), lax.axis_index("tvoc"), lax.axis_index("svoc")
-    n_d = 2
-    n = n_t * n_s
-    me = i * n_s + j
-    other = n_d - 1 - d
-    tokens, width = hidden.shape
-    shard = weight.shape[1]
-    per_owner = shard // blk
-    half = width // n_d
-    rows = width // n
-
-    loads = [
-        pltpu.make_async_copy(src, dst, load_sem.at[k])
-        for k, (src, dst) in enumerate(
-            ((hidden_hbm, hidden), (weight_hbm, weight))
-        )
-    ]
-    for load in loads:
-        load.start()
-
-    def peer(q):
-        r = lax.rem(me + q, n)
-        return r, {"tvoc": r // n_s, "svoc": lax.rem(r, n_s)}
-
-    barrier = pltpu.get_barrier_semaphore()
-
-    def greet(q, carry):
-        pl.semaphore_signal(barrier, inc=1, device_id=peer(q)[1], device_id_type=MESH)
-        return carry
-
-    lax.fori_loop(1, n, greet, 0)
-    pl.semaphore_signal(barrier, inc=1, device_id={"dp": other}, device_id_type=MESH)
-
-    for load in loads:
-        load.wait()
-    depth = 4 * blk
-    logits[...] = jnp.zeros_like(logits)
-
-    def logit_step(k, carry):
-        at = pl.multiple_of(k * depth, depth)
-        logits[...] += jnp.dot(hidden[:, pl.ds(at, depth)], weight[pl.ds(at, depth), :], preferred_element_type=f32)
-        return carry
-
-    lax.fori_loop(0, width // depth, logit_step, 0)
+        return carry
+
+    lax.fori_loop(0, n_t, pack, 0)
 
     pl.semaphore_wait(barrier, n)
 
@@ -144,7 +132,26 @@
         return carry
 
     lax.fori_loop(1, n_t, pack_send, 0)
+    loads[1].wait()
     hidden_copy().start()
+
+    loads[2].wait()
+    depth = 4 * blk
+    logits[...] = jnp.zeros_like(logits)
+
+    def logit_step(k, carry):
+        at = pl.multiple_of(k * depth, depth)
+        logits[...] += jnp.dot(hidden[:, pl.ds(at, depth)], weight[pl.ds(at, depth), :], preferred_element_type=f32)
+        return carry
+
+    lax.fori_loop(0, width // depth, logit_step, 0)
+
+    lg = logits[...]
+    top = jnp.max(lg, axis=1, keepdims=True)
+    e = jnp.exp(lg - top)
+    e_sum = jnp.sum(e, axis=1, keepdims=True)
+    shifted[...] = e
+
 
     own_at = d * half
 
@@ -177,12 +184,10 @@
 
     lg = logits[...]
     tm = mass[...]
-    top = jnp.max(lg, axis=1, keepdims=True)
-    e = jnp.exp(lg - top)
     positive = tm > 0
     parts = (
         top,
-        jnp.sum(e, axis=1, keepdims=True),
+        e_sum,
         jnp.sum(tm, axis=1, keepdims=True),
         jnp.sum(jnp.where(positive, tm * jnp.log(jnp.where(positive, tm, 1.0)), 0.0), axis=1, keepdims=True),
         jnp.sum(tm * lg, axis=1, keepdims=True),
@@ -192,7 +197,6 @@
     for k, part in enumerate(parts):
         wide = jnp.where(spot == k, part, wide)
     stats[me] = wide.T[0:8]
-    logits[...] = e
 
     def stat_copy(q, src):
         r, where = peer(q)
@@ -231,7 +235,7 @@
     rows8 = lax.broadcasted_iota(jnp.int32, (128, tokens), 0)
     back = jnp.where(rows8 == 0, largest, jnp.where(rows8 == 1, loss_scale / total, loss_scale / mass_sum)).T
     factor = jnp.exp(top - back[:, 0:1]) * back[:, 1:2]
-    g = logits[...] * factor - mass[...] * back[:, 2:3]
+    g = shifted[...] * factor - mass[...] * back[:, 2:3]
     grads[0:tokens, :] = g.astype(bf16)
     lg_copy = pltpu.make_async_remote_copy(
         src_ref=grads.at[pl.ds(0, tokens)], dst_ref=grads.at[pl.ds(tokens, tokens)],
@@ -240,17 +244,22 @@
     lg_copy.start()
     grad_t[...] = g.T.astype(bf16)
 
-    tile = 2 * blk
-
-    def gh_step(k, carry):
-        at = pl.multiple_of(k * tile, tile)
-        gh_t[pl.ds(at, tile), :] = jnp.dot(weight[pl.ds(at, tile), :], grad_t[...], preferred_element_type=f32)
-        return carry
-
-    lax.fori_loop(0, width // tile, gh_step, 0)
+    direct = rows % 16 == 0
+    if not direct:
+        tile = 2 * blk
+
+        def gh_step(k, carry):
+            at = pl.multiple_of(k * tile, tile)
+            gh_t[pl.ds(at, tile), :] = jnp.dot(weight[pl.ds(at, tile), :], grad_t[...], preferred_element_type=f32)
+            return carry
+
+        lax.fori_loop(0, width // tile, gh_step, 0)
 
     def chunk(ii, jj):
-        return gh_t[pl.ds(pl.multiple_of((ii * n_s + jj) * rows, 8), rows), :]
+        start = (ii * n_s + jj) * rows
+        if not direct:
+            return gh_t[pl.ds(pl.multiple_of(start, 8), rows), :]
+        return jnp.dot(weight[pl.ds(pl.multiple_of(start, 16), rows), :], grad_t[...], preferred_element_type=f32)
 
     def copy1(ii, jj, src):
         return pltpu.make_async_remote_copy(
@@ -277,18 +286,27 @@
 
     lax.fori_loop(1, n_s + 1, send1, 0)
 
+    def own_chunk(p, carry):
+        jj = lax.rem(j + p, n_s)
+        own_t[jj] = chunk(i, jj)
+        return carry
+
+    lax.fori_loop(1, n_s + 1, own_chunk, 0)
+
     lg_copy.wait_recv()
 
+    tall = 2 * blk
+
     def gw_step(k, carry):
-        at = pl.multiple_of(k * blk, blk)
-        gw_ref[pl.ds(at, blk), :] = jnp.dot(
-            hid_t[pl.ds(at, blk), :], grads[...], preferred_element_type=f32).astype(bf16)
-        return carry
-
-    lax.fori_loop(0, half // blk, gw_step, 0)
+        at = pl.multiple_of(k * tall, tall)
+        gw_ref[pl.ds(at, tall), :] = jnp.dot(
+            hid_t[pl.ds(at, tall), :], grads[...], preferred_element_type=f32).astype(bf16)
+        return carry
+
+    lax.fori_loop(0, half // tall, gw_step, 0)
 
     def gather1(jj):
-        acc = chunk(i, jj)
+        acc = own_t[jj]
         for q in range(1, n_t):
             ii = lax.rem(i + q, n_t)
             copy1(ii, jj, ii).wait_recv()
@@ -353,21 +371,6 @@
     hbm = pl.BlockSpec(memory_space=pltpu.HBM)
     DMA = pltpu.SemaphoreType.DMA
     parcel = (n_t, tokens + tag_rows, cap * blk)
-    packed = pl.pallas_call(
-        functools.partial(packer, n_t, shard // blk),
-        out_shape=jax.ShapeDtypeStruct(parcel, bf16),
-        in_specs=[smem, smem, vmem, hbm, hbm],
-        out_specs=vmem,
-        scratch_shapes=[
-            pltpu.VMEM(teacher_probs.shape, bf16),
-            pltpu.VMEM(block_values.shape[2:], bf16),
-            pltpu.VMEM((slots, tokens, blk), f32),
-            pltpu.VMEM((slots, lanes), f32),
-            pltpu.VMEM((n_t * cap, lanes), f32),
-            DMA((2,)),
-        ],
-        compiler_params=pltpu.CompilerParams(vmem_limit_bytes=32 * 1024 * 1024),
-    )(block_index, block_count, block_index, teacher_probs, block_values)
     div, gw, gh = pl.pallas_call(
         functools.partial(kernel, n_t, n_s, blk),
         out_shape=(
@@ -375,30 +378,38 @@
             jax.ShapeDtypeStruct((half, shard), bf16),
             jax.ShapeDtypeStruct((rows, tokens), f32),
         ),
-        in_specs=[vmem, hbm, hbm],
+        in_specs=[smem, smem, hbm, hbm, hbm, hbm],
         out_specs=(vmem, vmem, vmem),
         scratch_shapes=[
+            pltpu.VMEM((teacher_probs.shape[1] // blk, tokens, blk), bf16),
+            pltpu.VMEM(block_values.shape[2:], bf16),
             pltpu.VMEM(hidden.shape, bf16),
             pltpu.VMEM(student_weight.shape, bf16),
             pltpu.VMEM((tokens, half), bf16),
             pltpu.VMEM((half, 2 * tokens), bf16),
+            pltpu.VMEM((slots, tokens, blk), f32),
+            pltpu.VMEM((slots, lanes), f32),
+            pltpu.VMEM((n_t * cap, lanes), f32),
             pltpu.VMEM(parcel, bf16),
+            pltpu.VMEM(parcel, bf16),
+            pltpu.VMEM((tokens, shard), f32),
             pltpu.VMEM((tokens, shard), f32),
             pltpu.VMEM((tokens, shard), f32),
             pltpu.VMEM((n, 8, tokens), f32),
             pltpu.VMEM((2 * tokens, shard), bf16),
             pltpu.VMEM((shard, tokens), bf16),
             pltpu.VMEM((width, tokens), f32),
+            pltpu.VMEM((n_s, rows, tokens), f32),
             pltpu.VMEM((n_t, n_s, rows, tokens), bf16),
             pltpu.VMEM((n_t, n_s, rows, tokens), bf16),
             pltpu.VMEM((n_s, rows, tokens), bf16),
             pltpu.VMEM((n_s, rows, tokens), bf16),
-            DMA((2,)), DMA((2,)), DMA((n_t,)), DMA((n_t,)), DMA((n,)), DMA((n,)), DMA((2,)),
+            DMA((teacher_probs.shape[1] // blk,)), DMA((3,)), DMA((2,)), DMA((n_t,)), DMA((n_t,)), DMA((n,)), DMA((n,)), DMA((2,)),
             DMA((n_t, n_s)), DMA((n_t, n_s)), DMA((n_s,)), DMA((n_s,)),
         ],
         compiler_params=pltpu.CompilerParams(
-            collective_id=0, has_side_effects=True, vmem_limit_bytes=32 * 1024 * 1024),
-    )(packed, hidden, student_weight)
+            collective_id=0, has_side_effects=True, vmem_limit_bytes=67043328 - 7 * 2**18),
+    )(jnp.swapaxes(block_index, 2, 3), block_count, teacher_probs, block_values, hidden, student_weight)
     return div.reshape(tokens), gw, gh.T
 
 

time: 43.3 us -> 37.3 us (0.86)
  Pallas kernels: 34.4 us -> 31.4 us
  local copies, waits for them, and re-layouts: 7.39 us -> 4.47 us
    unnamed x12 -> x5, local copies, waits for them, and re-layouts: 7.39 us -> 4.47 us
    pallas_call x1 -> x0, Pallas kernels: 2.78 us -> none  [local(): pl.pallas_call(functools.partial(packer, n_t, shard // blk), out_shape=ja...]
where the time goes in v2:
time: 37.3 us; the launch traced here: 37.2 us
  Pallas kernels  31.4 us (84%)
  local copies, waits for them, and re-layouts  4.47 us (12%)
  between operations  1.29 us (3%)
    pallas_call x1, Pallas kernels, local(): pl.pallas_call(functools.partial(kernel, n_t, n_s, blk), out_shape=(jax.S...  31.4 us
    unnamed x5, local copies, waits for them, and re-layouts  4.47 us

profile of v2, /device:TPU:0, one launch (start us, length us, event | category | flops | bytes accessed | tf_op | source)
XLA Modules:
  0.0 37.2 jit_solution(8780617225290928595)
XLA Ops:
  1.3 31.4 %shard_map.85 = (f32[1,128]{1,0:T(1,128)}, bf16[1536,512]{1,0:T(8,128)(2,1)}, f32[192,128]{1,0:T(8,128)}) custom-call(s32[1,1,2,24]{3,2,1,0:T(2,128)} %bitcast.4, s32[1,1]{1,0:T(1,128)S(6)} %copy.12.cnt_s, bf16[128,5120]{1,0:T(8,128)(2,1)} %teacher_hbm.1, bf16[1,1,24,128,128]{4,3,2,1,0:T(8,128)(2,1)} %values_hbm.1, bf16[128,3072]{1,0:T(8,128)(2,1)} %hidden_hbm.1, ...), custom_call_target="tpu_custom_call" | custom-call | tf_op jit(solution)/shard_map/pallas_call | solution.py:374
  32.7 1.1 %copy.13 = f32[128]{0:T(128)} copy(f32[128]{0:T(128)} %bitcast.5) | data formatting | bytes 1024
  33.8 0.0 copy-start
  33.8 2.7 %copy.14 = bf16[1536,512]{1,0:T(8,128)(2,1)} copy(bf16[1536,512]{1,0:T(8,128)(2,1)} %get-tuple-element.13) | data formatting | bytes 3145728
  36.5 0.0 copy-done
  36.5 0.6 %copy.15 = f32[128,192]{0,1:T(8,128)} copy(f32[128,192]{0,1:T(8,128)S(1)} %bitcast.3) | data formatting | bytes 196608
Async XLA Ops:
  33.8 2.7 %copy-start = (f32[192,128]{1,0:T(8,128)S(1)}, f32[192,128]{1,0:T(8,128)}, u32[]{:S(2)}) copy-start(f32[192,128]{1,0:T(8,128)} %get-tuple-element.8) | copy-start | bytes 294916

commit v3 on v2

--- a/solution.py
+++ b/solution.py
@@ -109,7 +109,7 @@
                 tags[pl.ds(o * cap + k, 1), 0:blk], (tag_rows, blk)).astype(bf16)
         return carry
 
-    lax.fori_loop(0, n_t, pack, 0)
+    lax.fori_loop(1, n_t, pack, 0)
 
     pl.semaphore_wait(barrier, n)
 
@@ -134,6 +134,7 @@
     lax.fori_loop(1, n_t, pack_send, 0)
     loads[1].wait()
     hidden_copy().start()
+    pack(0, 0)
 
     loads[2].wait()
     depth = 4 * blk
@@ -359,6 +360,17 @@
         return carry
 
     lax.fori_loop(1, n_s, drain2, 0)
+
+
+def flush(div, gw, gh, div_out, gw_out, gh_out, sem):
+    copies = [
+        pltpu.make_async_copy(src, dst, sem.at[k])
+        for k, (src, dst) in enumerate(((gw, gw_out), (gh, gh_out), (div, div_out)))
+    ]
+    for copy in copies:
+        copy.start()
+    for copy in copies:
+        copy.wait()
 
 
 def local(n_t, n_s, teacher_probs, block_values, block_index, block_count, hidden, student_weight):
@@ -408,8 +420,18 @@
             DMA((n_t, n_s)), DMA((n_t, n_s)), DMA((n_s,)), DMA((n_s,)),
         ],
         compiler_params=pltpu.CompilerParams(
-            collective_id=0, has_side_effects=True, vmem_limit_bytes=67043328 - 7 * 2**18),
-    )(jnp.swapaxes(block_index, 2, 3), block_count, teacher_probs, block_values, hidden, student_weight)
+            collective_id=0, has_side_effects=True, vmem_limit_bytes=32 * 1024 * 1024),
+    )(
+        pltpu.with_memory_space_constraint(jnp.swapaxes(block_index, 2, 3), pltpu.HBM), block_count,
+        *(pltpu.with_memory_space_constraint(x, pltpu.HBM) for x in (teacher_probs, block_values, hidden, student_weight)))
+    div, gw, gh = pl.pallas_call(
+        flush,
+        out_shape=tuple(jax.ShapeDtypeStruct(x.shape, x.dtype) for x in (div, gw, gh)),
+        in_specs=[vmem] * 3,
+        out_specs=(hbm,) * 3,
+        scratch_shapes=[DMA((3,))],
+        compiler_params=pltpu.CompilerParams(vmem_limit_bytes=2**20),
+    )(div, gw, gh)
     return div.reshape(tokens), gw, gh.T
 
 

time: 37.3 us -> 32.9 us (0.88)
  local copies, waits for them, and re-layouts: 4.47 us -> 0 us
    unnamed x5 -> x0, local copies, waits for them, and re-layouts: 4.47 us -> none
    pallas_call x0 -> x1, Pallas kernels: none -> 1.19 us  [local(): pl.pallas_call(flush, out_shape=tuple((jax.ShapeDtypeStruct(x.shape, x.dt...]
    pallas_call x1, Pallas kernels: 31.4 us -> 30.2 us  [local(): pl.pallas_call(functools.partial(kernel, n_t, n_s, blk), out_shape=(jax.S...]
where the time goes in v3:
time: 32.9 us; the launch traced here: 32.7 us
  Pallas kernels  31.4 us (95%)
  between operations  1.29 us (4%)
    pallas_call x1, Pallas kernels, local(): pl.pallas_call(functools.partial(kernel, n_t, n_s, blk), out_shape=(jax.S...  30.2 us
    pallas_call x1, Pallas kernels, local(): pl.pallas_call(flush, out_shape=tuple((jax.ShapeDtypeStruct(x.shape, x.dt...  1.19 us

profile of v3, /device:TPU:0, one launch (start us, length us, event | category | flops | bytes accessed | tf_op | source)
XLA Modules:
  0.0 32.7 jit_solution(5182986100618763320)
XLA Ops:
  1.3 30.2 %shard_map.85 = (f32[1,128]{1,0:T(1,128)S(1)}, bf16[1536,512]{1,0:T(8,128)(2,1)S(1)}, f32[192,128]{1,0:T(8,128)S(1)}) custom-call(s32[1,1,2,24]{3,2,1,0:T(2,128)} %bitcast.3, s32[1,1]{1,0:T(1,128)S(6)} %copy.9.cnt_s, bf16[128,5120]{1,0:T(8,128)(2,1)} %teacher_hbm.1, bf16[1,1,24,128,128]{4,3,2,1,0:T(8,128)(2,1)} %values_hbm.1, bf16[128,3072]{1,0:T(8,128)(2,1)} %hidden_hbm.1, ...), custom_call_target="tpu_custom_call" | custom-call | tf_op jit(solution)/shard_map/pallas_call | solution.py:386
  31.5 1.2 %shard_map.86 = (f32[1,128]{1,0:T(1,128)}, bf16[1536,512]{1,0:T(8,128)(2,1)}, f32[192,128]{1,0:T(8,128)}) custom-call(f32[1,128]{1,0:T(1,128)S(1)} %get-tuple-element.9.div, bf16[1536,512]{1,0:T(8,128)(2,1)S(1)} %get-tuple-element.10.gw, f32[192,128]{1,0:T(8,128)S(1)} %get-tuple-element.11.gh), custom_call_target="tpu_custom_call" | custom-call | tf_op jit(solution)/shard_map/pallas_call | solution.py:427
